TPU v7x, 128 devices: a whole 4x4x4 slice. The times are simulated.
128 devices in a mesh: seq: 16 (over z, x), head: 8 (over y, core).
Axes of the slice: x: 4, y: 4, z: 4, core: 2. Of those that a mesh axis runs over, the one named last changes fastest.
Arguments:
- context: bfloat16 [32768, 2048], P('seq'), may hold values from -64 to 64
- wq_cross: bfloat16 [2048, 2048], P(None, 'head'), may hold values from -4 to 4
- wk_cross: bfloat16 [2048, 2048], P(None, 'head'), may hold values from -4 to 4
- wv_cross: bfloat16 [2048, 2048], P(None, 'head'), may hold values from -0.125 to 0.125
- wo_cross: bfloat16 [2048, 2048], P('head'), may hold values from -0.125 to 0.125
- wq_latent: bfloat16 [2048, 2048], P(None, 'head'), may hold values from -4 to 4
- wk_latent: bfloat16 [2048, 2048], P(None, 'head'), may hold values from -4 to 4
- wv_latent: bfloat16 [2048, 2048], P(None, 'head'), may hold values from -0.125 to 0.125
- wo_latent: bfloat16 [2048, 2048], P('head'), may hold values from -0.125 to 0.125
- cross_keep: int32 [16, 2048, 4096], P('head', None, 'seq'), may hold values from 0 to 255, as said below
- latent_keep: int32 [16, 2048, 128], P('head'), may hold values from 0 to 65535, as said below
- residual_keep: int32 [2, 2048, 128], replicated, may hold values from 0 to 65535, as said below
Outputs:
- latents_out: bfloat16 [2048, 2048], P('seq', 'head')
Inputs may be any that keep to these rules, and one draw needn't show every extreme that they name: `cross_keep`: each of the 8 low bits of a word is one keep flag, laid out as the steps say. `latent_keep`: each of the 16 low bits of a word is one keep flag, laid out as the steps say. `residual_keep`: each of the 16 low bits of a word is one keep flag, laid out as the steps say.
All inputs are finite; a program needn't handle non-finite values.
Results may differ from a plain program's by a relative error of at most 0.015.
Values may be sent and summed in bfloat16 or wider, within the bound.
No kernel may reach another device: no remote copies, remote signals or barrier semaphores. Data moves between devices by JAX's collectives and lax.ppermute only.
A program may use at most 128 MiB of HBM per device.

v0:
```python
import math
import jax
import jax.numpy as jnp
from jax import lax
from jax.sharding import PartitionSpec as P

keep_scale = 8.0 / 7.0
masked = -1e30


def from_root(value, axis, source):
    kept = jnp.where(lax.axis_index(axis) == source, value, 0).astype(value.dtype)
    return lax.psum(kept, axis)


def copy_for_each(value, axis):
    size = lax.axis_size(axis)
    return lax.all_to_all(
        jnp.broadcast_to(value[None], (size, *value.shape)), axis, 0, 0, tiled=True
    )


def of_everyone(value, axis):
    everything = copy_for_each(value, axis)
    return jnp.max(everything, axis=0)


def side_by_side(arrays, axis, dim, along):
    widths = [math.prod(a.shape[along:]) for a in arrays]
    both = jnp.concatenate(
        [a.reshape(*a.shape[:along], w) for a, w in zip(arrays, widths)], axis=along
    )
    filled = lax.psum_scatter(both, axis, scatter_dimension=dim, tiled=True)
    parts = jnp.split(filled, [sum(widths[:k]) for k in range(1, len(widths))], axis=along)
    return tuple(
        (b.reshape(*filled.shape[:along], *a.shape[along:]) for a, b in zip(arrays, parts))
    )


def in_blocks(value, dim, size):
    before, after = (value.shape[:dim], value.shape[dim + 1 :])
    return jnp.moveaxis(value.reshape(*before, size, -1, *after), dim, 0)


def sum_at_owner(value, axis, dim):
    parts = in_blocks(value, dim, lax.axis_size(axis))
    arrived = lax.all_to_all(parts, axis, split_axis=0, concat_axis=0, tiled=True)
    return arrived.astype(jnp.float32).sum(axis=0)


def of_everyone_2(value, axis):
    return copy_for_each(value, axis).sum(axis=0)


def laid_out(parts, dim):
    shape = list(parts.shape[1:])
    shape[dim] *= parts.shape[0]
    return jnp.moveaxis(parts, 0, dim).reshape(shape)


def gather_directly(value, axis, dim):
    parts = copy_for_each(value, axis)
    return laid_out(parts, dim)


def side_by_side_2(arrays, axis, dim, along):
    widths = [a.shape[along] for a in arrays]
    both = jnp.concatenate(arrays, axis=along)
    filled = lax.all_gather(both, axis, axis=dim, tiled=True)
    return tuple(jnp.split(filled, [sum(widths[:k]) for k in range(1, len(widths))], axis=along))


def unpack_bits(packed_words, word_bits):
    shifts = jnp.arange(word_bits, dtype=jnp.int32)
    bit_table = jnp.bitwise_and(jnp.right_shift(packed_words[..., None, :], shifts[:, None]), 1)
    return bit_table.reshape(packed_words.shape[:-1] + (word_bits * packed_words.shape[-1],))


def rms_rows(matrix):
    wide_rows = matrix.astype(jnp.float32)
    mean_square = jnp.mean(wide_rows * wide_rows, axis=-1, keepdims=True)
    return (wide_rows * lax.rsqrt(mean_square + 1e-06)).astype(jnp.bfloat16)


def per_device(
    context,
    wq_cross,
    wk_cross,
    wv_cross,
    wo_cross,
    wq_latent,
    wk_latent,
    wv_latent,
    wo_latent,
    cross_keep,
    latent_keep,
    residual_keep,
):
    seq_count = lax.axis_size("seq")
    seq_index = lax.axis_index("seq")
    head_index = lax.axis_index("head")
    tok_rows, model_width = context.shape
    head_local = cross_keep.shape[0]
    latent_count = cross_keep.shape[1]
    head_dim = wq_cross.shape[1] // head_local
    query_width = head_local * head_dim
    columns = model_width // lax.axis_size("head")
    local_rows = latent_count // seq_count
    score_scale = 1.0 / math.sqrt(head_dim)
    normed = rms_rows(context)
    key_rows = jnp.dot(normed, wk_cross, preferred_element_type=jnp.float32).astype(jnp.bfloat16)
    value_rows = jnp.dot(normed, wv_cross, preferred_element_type=jnp.float32).astype(jnp.bfloat16)
    own_queries = jnp.dot(normed, wq_cross, preferred_element_type=jnp.float32).astype(jnp.bfloat16)
    own_columns = lax.dynamic_slice_in_dim(context, head_index * columns, columns, 1)
    outgoing_rows = jnp.concatenate([own_queries, own_columns], axis=1)
    arrived_rows = from_root(outgoing_rows, "seq", seq_count - 1)
    queries = arrived_rows[:, :query_width]
    latent_context = arrived_rows[:, query_width:]
    first_latent = (seq_count - 1) * tok_rows
    block_rows = min(512, latent_count)
    block_count = latent_count // block_rows
    query_blocks = queries.reshape(block_count, block_rows, head_local, head_dim)
    mask_blocks = cross_keep.reshape(head_local, block_count, block_rows, -1).transpose(1, 0, 2, 3)
    key_heads = key_rows.reshape(tok_rows, head_local, head_dim)
    value_heads = value_rows.reshape(tok_rows, head_local, head_dim)
    key_pos = seq_index * tok_rows + jnp.arange(tok_rows, dtype=jnp.int32)

    def cross_block(block_items):
        query_block, mask_block, number = block_items
        scores = (
            jnp.einsum("qhd,khd->hqk", query_block, key_heads, preferred_element_type=jnp.float32)
            * score_scale
        )
        query_pos = first_latent + number * block_rows + jnp.arange(block_rows, dtype=jnp.int32)
        allowed = key_pos[None, None, :] <= query_pos[None, :, None]
        scores = jnp.where(allowed, scores, masked)
        row_top = jnp.max(scores, axis=-1)
        exponent = jnp.where(allowed, jnp.exp(scores - row_top[..., None]), 0.0)
        row_sum = jnp.sum(exponent, axis=-1)
        keep_flags = unpack_bits(mask_block, 8).astype(jnp.float32)
        weights = (exponent * keep_flags * keep_scale).astype(jnp.bfloat16)
        summed = jnp.einsum(
            "hqk,khd->hqd", weights, value_heads, preferred_element_type=jnp.float32
        )
        return (summed, row_top, row_sum)

    summed, row_top, row_sum = lax.map(
        cross_block, (query_blocks, mask_blocks, jnp.arange(block_count, dtype=jnp.int32))
    )
    summed = summed.transpose(1, 0, 2, 3).reshape(head_local, latent_count, head_dim)
    row_top = row_top.transpose(1, 0, 2).reshape(head_local, latent_count)
    row_sum = row_sum.transpose(1, 0, 2).reshape(head_local, latent_count)
    first_row = seq_index * local_rows
    row_peak = of_everyone(row_top, "seq")
    factor = jnp.exp(row_top - row_peak)
    numerator, denominator = tuple(
        (
            part.astype(jnp.float32)
            for part in side_by_side(
                (
                    (summed * factor[..., None]).astype(jnp.bfloat16),
                    (row_sum * factor).astype(jnp.bfloat16),
                ),
                "seq",
                1,
                2,
            )
        )
    )
    attended_heads = numerator / denominator[..., None]
    attended = (
        attended_heads.transpose(1, 0, 2)
        .reshape(local_rows, head_local * head_dim)
        .astype(jnp.bfloat16)
    )
    inputs = lax.dynamic_slice_in_dim(latent_context, first_row, local_rows, 0).astype(jnp.float32)
    residual_rows = lax.dynamic_slice_in_dim(residual_keep, first_row, local_rows, 1)
    residual_mask = lax.dynamic_slice_in_dim(
        unpack_bits(residual_rows, 16), head_index * columns, columns, 2
    ).astype(jnp.float32)
    branch = jnp.dot(attended, wo_cross, preferred_element_type=jnp.float32)
    branch = sum_at_owner(branch.astype(jnp.bfloat16), "head", 1)
    latents = (inputs + residual_mask[0] * keep_scale * branch).astype(jnp.bfloat16)
    wide_latents = latents.astype(jnp.float32)
    squares = of_everyone_2(jnp.sum(wide_latents * wide_latents, axis=-1), "head")
    normed_columns = (wide_latents * lax.rsqrt(squares / model_width + 1e-06)[:, None]).astype(
        jnp.bfloat16
    )
    normed_latents = gather_directly(normed_columns, "head", 1)
    latent_queries = jnp.dot(normed_latents, wq_latent, preferred_element_type=jnp.float32).astype(
        jnp.bfloat16
    )
    latent_keys = jnp.dot(normed_latents, wk_latent, preferred_element_type=jnp.float32).astype(
        jnp.bfloat16
    )
    latent_values = jnp.dot(normed_latents, wv_latent, preferred_element_type=jnp.float32).astype(
        jnp.bfloat16
    )
    my_index = first_row + jnp.arange(local_rows, dtype=jnp.int32)
    latent_words = lax.dynamic_slice_in_dim(latent_keep, first_row, local_rows, 1)
    latent_mask = unpack_bits(latent_words, 16).astype(jnp.float32)
    query_heads = latent_queries.reshape(local_rows, head_local, head_dim)
    initial = (
        jnp.zeros((head_local, local_rows, head_dim), jnp.float32),
        jnp.full((head_local, local_rows), masked, jnp.float32),
        jnp.zeros((head_local, local_rows), jnp.float32),
    )
    key_piece, value_piece = side_by_side_2((latent_keys, latent_values), "seq", 0, 1)
    piece_rows = key_piece.shape[0]
    key_index = jnp.arange(piece_rows, dtype=jnp.int32)

    def update(current):
        weighted, old_top, old_sum = current
        scores = (
            jnp.einsum(
                "qhd,khd->hqk",
                query_heads,
                key_piece.reshape(piece_rows, head_local, head_dim),
                preferred_element_type=jnp.float32,
            )
            * score_scale
        )
        allowed = key_index[None, None, :] <= my_index[None, :, None]
        scores = jnp.where(allowed, scores, masked)
        new_top = jnp.maximum(old_top, jnp.max(scores, axis=-1))
        exponent = jnp.where(allowed, jnp.exp(scores - new_top[..., None]), 0.0)
        keep_flags = jnp.take(latent_mask, key_index, axis=2)
        weights = (exponent * keep_flags * keep_scale).astype(jnp.bfloat16)
        added = jnp.einsum(
            "hqk,khd->hqd",
            weights,
            value_piece.reshape(piece_rows, head_local, head_dim),
            preferred_element_type=jnp.float32,
        )
        return (added, new_top, jnp.sum(exponent, axis=-1))

    needed = jnp.min(key_index) <= jnp.max(my_index)
    weighted, latent_top, latent_sum = lax.cond(needed, update, lambda current: current, initial)
    latent_attended = (
        (weighted / latent_sum[..., None])
        .transpose(1, 0, 2)
        .reshape(local_rows, head_local * head_dim)
        .astype(jnp.bfloat16)
    )
    latent_branch = jnp.dot(latent_attended, wo_latent, preferred_element_type=jnp.float32)
    latent_branch = sum_at_owner(latent_branch.astype(jnp.bfloat16), "head", 1)
    result = (wide_latents + residual_mask[1] * keep_scale * latent_branch).astype(jnp.bfloat16)
    return result


def solution(mesh):
    in_specs = (
        P("seq", None),
        P(None, "head"),
        P(None, "head"),
        P(None, "head"),
        P("head", None),
        P(None, "head"),
        P(None, "head"),
        P(None, "head"),
        P("head", None),
        P("head", None, "seq"),
        P("head", None, None),
        P(),
    )
    out_specs = P("seq", "head")
    return jax.shard_map(
        per_device, mesh=mesh, in_specs=in_specs, out_specs=out_specs, check_vma=False
    )
```

profile of v0, /device:TPU:1, one launch (start us, length us, event | category | flops | bytes accessed | tf_op | source)
XLA Modules:
  0.0 501.3 jit_solution(15853030671720512966)
XLA Ops:
  6.5 5.2 %fusion.31 = f32[2048]{0:T(1024)S(1)} fusion(bf16[2048,2048]{1,0:T(8,128)(2,1)} %param.16), kind=kLoop, calls=%fused_computation.50 | loop fusion | flops 12580864 | bytes 8396800 | tf_op jit(solution)/shard_map/reduce_sum | solution.py:81
  13.7 5.9 %convolution_convert_fusion.2 = bf16[2048,256]{0,1:T(8,128)(2,1)S(1)} fusion(bf16[2048,256]{1,0:T(8,128)(2,1)S(1)} %copy-done, bf16[2048,2048]{1,0:T(8,128)(2,1)} %param.16, f32[2048]{0:T(1024)S(1)} %add_rsqrt_fusion), kind=kOutput, calls=%fused_computation.54 | convolution fusion | flops 2160590848 | bytes 10493952 | tf_op jit(solution)/shard_map/dot_general | solution.py:113
  19.6 1.7 maximum_select_fusion
  21.6 6.2 %convolution_convert_fusion.1 = bf16[2048,256]{0,1:T(8,128)(2,1)S(1)} fusion(bf16[2048,256]{1,0:T(8,128)(2,1)} %param.18, bf16[2048,2048]{1,0:T(8,128)(2,1)} %param.16, f32[2048]{0:T(1024)S(1)} %add_rsqrt_fusion), kind=kOutput, calls=%fused_computation.53 | convolution fusion | flops 2160590848 | bytes 10493952 | tf_op jit(solution)/shard_map/dot_general | solution.py:111
  29.2 5.9 %convolution_convert_fusion = bf16[2048,256]{0,1:T(8,128)(2,1)S(1)} fusion(bf16[2048,256]{1,0:T(8,128)(2,1)S(1)} %copy-done.10, bf16[2048,2048]{1,0:T(8,128)(2,1)} %param.16, f32[2048]{0:T(1024)S(1)} %add_rsqrt_fusion), kind=kOutput, calls=%fused_computation.52 | convolution fusion | flops 2160590848 | bytes 10493952 | tf_op jit(solution)/shard_map/dot_general | solution.py:112
  36.4 78.3 %all-reduce.2.cloned.1.call-done = bf16[2048,512]{0,1:T(8,128)(2,1)} async-done(((bf16[2048,512]{0,1:T(8,128)(2,1)}), bf16[2048,512]{0,1:T(8,128)(2,1)}) %all-reduce.2.cloned.1.call-update) | async-done | bytes 2097168 | tf_op jit(solution)/shard_map/psum | solution.py:13
  114.7 2.7 fusion.58
  118.2 1.7 copy.129
  119.9 143.6 %while.15 = (s32[]{:T(128)}, f32[4,2,512,128]{3,2,0,1:T(8,128)}, f32[4,2,512]{2,1,0:T(2,128)S(1)}, f32[4,2,512]{2,1,0:T(2,128)S(1)}, s32[4]{0:T(128)S(1)}, /*ind...) while((s32[]{:T(128)}, f32[4,2,512,128]{3,2,0,1:T(8,128)}, ...), condition=%wide.region_5.6_spmd.clone, body=%wide.region_2.5_spmd.clone.sunk | while | flops 1112539648 | bytes 102584528 | solution.py:147
  121.2 3.8 shift_right_arithmetic.114
  125.0 9.3 %shift_right_arithmetic.115 = s32[2,512,2048]{2,1,0:T(8,128)} reshape(s32[2,512,8,256]{3,2,1,0:T(8,128)} %shift_right_arithmetic.114) | data formatting | bytes 16777216 | tf_op jit(solution)/shard_map/while/body/eval_jaxpr/shift_right_arithmetic | solution.py:75
  136.1 6.6 %fusion.84 = (f32[2,512]{1,0:T(2,128)S(1)}, f32[2,512,2048]{2,1,0:T(8,128)}) fusion(pred[512,2048]{1,0:T(8,128)(4,1)S(1)} %broadcast_compare_fusion.3, bf16[2048,2,128]{2,0,1:T(8,128)(2,1)} %get-tuple-element.350, bf16[4,512,2,128]{3,1,2,0:T(8,128)(2,1)} %get-tuple-element.349, s32[]{:T(128)S(6)} %copy.189), kind=kOutput, calls=%fused_computation.26.clone.1 | convolution fusion | flops 543161344 | bytes 10752004 | tf_op jit(solution)/shard_map/while/body/eval_jaxpr/qhd,khd->hqk/dot_general | solution.py:131
  142.8 8.0 %fusion.85 = f32[4,2,512,128]{3,2,0,1:T(8,128)} fusion(f32[4,2,512,128]{3,2,0,1:T(8,128)} %get-tuple-element.332, s32[]{:T(128)S(6)} %copy.189, bf16[2048,2,128]{2,0,1:T(8,128)(2,1)} %get-tuple-element.352, s32[2,512,2048]{2,1,0:T(8,128)S(1)} %copy-done.2, f32[2,512,2048]{2,1,0:T(8,128)} %get-tuple-element.314, s32[2048]{0:T(1024)S(1)} %bitcast.169, ...), kind=kOutput, calls=%fused_computation.32.clone.1 | convolution fusion | flops 557842432 | bytes 19410948 | tf_op jit(solution)/shard_map/while/body/eval_jaxpr/hqk,khd->hqd/dot_general | solution.py:142
  150.8 5.0 fusion.86
  157.2 3.8 shift_right_arithmetic.114
  160.9 9.3 %shift_right_arithmetic.115 = s32[2,512,2048]{2,1,0:T(8,128)} reshape(s32[2,512,8,256]{3,2,1,0:T(8,128)} %shift_right_arithmetic.114) | data formatting | bytes 16777216 | tf_op jit(solution)/shard_map/while/body/eval_jaxpr/shift_right_arithmetic | solution.py:75
  172.0 6.6 %fusion.84 = (f32[2,512]{1,0:T(2,128)S(1)}, f32[2,512,2048]{2,1,0:T(8,128)}) fusion(pred[512,2048]{1,0:T(8,128)(4,1)S(1)} %broadcast_compare_fusion.3, bf16[2048,2,128]{2,0,1:T(8,128)(2,1)} %get-tuple-element.350, bf16[4,512,2,128]{3,1,2,0:T(8,128)(2,1)} %get-tuple-element.349, s32[]{:T(128)S(6)} %copy.189), kind=kOutput, calls=%fused_computation.26.clone.1 | convolution fusion | flops 543161344 | bytes 10752004 | tf_op jit(solution)/shard_map/while/body/eval_jaxpr/qhd,khd->hqk/dot_general | solution.py:131
  178.7 8.0 %fusion.85 = f32[4,2,512,128]{3,2,0,1:T(8,128)} fusion(f32[4,2,512,128]{3,2,0,1:T(8,128)} %get-tuple-element.332, s32[]{:T(128)S(6)} %copy.189, bf16[2048,2,128]{2,0,1:T(8,128)(2,1)} %get-tuple-element.352, s32[2,512,2048]{2,1,0:T(8,128)S(1)} %copy-done.2, f32[2,512,2048]{2,1,0:T(8,128)} %get-tuple-element.314, s32[2048]{0:T(1024)S(1)} %bitcast.169, ...), kind=kOutput, calls=%fused_computation.32.clone.1 | convolution fusion | flops 557842432 | bytes 19410948 | tf_op jit(solution)/shard_map/while/body/eval_jaxpr/hqk,khd->hqd/dot_general | solution.py:142
  186.7 5.0 fusion.86
  193.1 3.8 shift_right_arithmetic.114
  196.9 9.3 %shift_right_arithmetic.115 = s32[2,512,2048]{2,1,0:T(8,128)} reshape(s32[2,512,8,256]{3,2,1,0:T(8,128)} %shift_right_arithmetic.114) | data formatting | bytes 16777216 | tf_op jit(solution)/shard_map/while/body/eval_jaxpr/shift_right_arithmetic | solution.py:75
  208.0 6.6 %fusion.84 = (f32[2,512]{1,0:T(2,128)S(1)}, f32[2,512,2048]{2,1,0:T(8,128)}) fusion(pred[512,2048]{1,0:T(8,128)(4,1)S(1)} %broadcast_compare_fusion.3, bf16[2048,2,128]{2,0,1:T(8,128)(2,1)} %get-tuple-element.350, bf16[4,512,2,128]{3,1,2,0:T(8,128)(2,1)} %get-tuple-element.349, s32[]{:T(128)S(6)} %copy.189), kind=kOutput, calls=%fused_computation.26.clone.1 | convolution fusion | flops 543161344 | bytes 10752004 | tf_op jit(solution)/shard_map/while/body/eval_jaxpr/qhd,khd->hqk/dot_general | solution.py:131
  214.6 8.0 %fusion.85 = f32[4,2,512,128]{3,2,0,1:T(8,128)} fusion(f32[4,2,512,128]{3,2,0,1:T(8,128)} %get-tuple-element.332, s32[]{:T(128)S(6)} %copy.189, bf16[2048,2,128]{2,0,1:T(8,128)(2,1)} %get-tuple-element.352, s32[2,512,2048]{2,1,0:T(8,128)S(1)} %copy-done.2, f32[2,512,2048]{2,1,0:T(8,128)} %get-tuple-element.314, s32[2048]{0:T(1024)S(1)} %bitcast.169, ...), kind=kOutput, calls=%fused_computation.32.clone.1 | convolution fusion | flops 557842432 | bytes 19410948 | tf_op jit(solution)/shard_map/while/body/eval_jaxpr/hqk,khd->hqd/dot_general | solution.py:142
  222.6 5.0 fusion.86
  229.0 3.8 shift_right_arithmetic.114
  232.8 9.3 %shift_right_arithmetic.115 = s32[2,512,2048]{2,1,0:T(8,128)} reshape(s32[2,512,8,256]{3,2,1,0:T(8,128)} %shift_right_arithmetic.114) | data formatting | bytes 16777216 | tf_op jit(solution)/shard_map/while/body/eval_jaxpr/shift_right_arithmetic | solution.py:75
  243.9 6.6 %fusion.84 = (f32[2,512]{1,0:T(2,128)S(1)}, f32[2,512,2048]{2,1,0:T(8,128)}) fusion(pred[512,2048]{1,0:T(8,128)(4,1)S(1)} %broadcast_compare_fusion.3, bf16[2048,2,128]{2,0,1:T(8,128)(2,1)} %get-tuple-element.350, bf16[4,512,2,128]{3,1,2,0:T(8,128)(2,1)} %get-tuple-element.349, s32[]{:T(128)S(6)} %copy.189), kind=kOutput, calls=%fused_computation.26.clone.1 | convolution fusion | flops 543161344 | bytes 10752004 | tf_op jit(solution)/shard_map/while/body/eval_jaxpr/qhd,khd->hqk/dot_general | solution.py:131
  250.5 8.0 %fusion.85 = f32[4,2,512,128]{3,2,0,1:T(8,128)} fusion(f32[4,2,512,128]{3,2,0,1:T(8,128)} %get-tuple-element.332, s32[]{:T(128)S(6)} %copy.189, bf16[2048,2,128]{2,0,1:T(8,128)(2,1)} %get-tuple-element.352, s32[2,512,2048]{2,1,0:T(8,128)S(1)} %copy-done.2, f32[2,512,2048]{2,1,0:T(8,128)} %get-tuple-element.314, s32[2048]{0:T(1024)S(1)} %bitcast.169, ...), kind=kOutput, calls=%fused_computation.32.clone.1 | convolution fusion | flops 557842432 | bytes 19410948 | tf_op jit(solution)/shard_map/while/body/eval_jaxpr/hqk,khd->hqd/dot_general | solution.py:142
  258.6 5.0 fusion.86
  263.7 11.5 %all_to_all.26 = f32[16,2,2048]{2,1,0:T(2,128)S(1)} all-to-all(f32[16,2,2048]{2,1,0:T(2,128)S(1)} %broadcast_in_dim.109), channel_id=1, replica_groups=mesh['seq'=16,'head'=8] {'seq'}, dimensions={0} | all-to-all | bytes 524288 | tf_op jit(solution)/shard_map/all_to_all | solution.py:18
  275.9 2.0 fusion.33
  277.9 1.8 pad_maximum_fusion
  279.7 74.6 %reduce-scatter.2.cloned.1.call-done = bf16[2,128,129]{2,1,0:T(8,128)(2,1)} async-done(((bf16[2,2048,129]{2,1,0:T(8,128)(2,1)}), bf16[2,128,129]{2,1,0:T(8,128)(2,1)}) %reduce-scatter.2.cloned.1.call-update) | async-done | bytes 66064 | tf_op jit(solution)/shard_map/reduce_scatter | solution.py:33
  357.6 6.6 %all-to-all-start.1 = ((bf16[8,128,256]{2,1,0:T(8,128)(2,1)}), bf16[8,128,256]{2,1,0:T(8,128)(2,1)S(1)}, u32[]{:S(2)}, u32[]{:S(2)}) async-start(bf16[8,128,256]{2,1,0:T(8,128)(2,1)} %bitcast.136), calls=%async_computation.2 | async-start | bytes 1048576 | tf_op jit(solution)/shard_map/all_to_all | solution.py:47
  365.8 7.7 %all-to-all-done.1 = bf16[8,128,256]{2,1,0:T(8,128)(2,1)S(1)} async-done(((bf16[8,128,256]{2,1,0:T(8,128)(2,1)}), bf16[8,128,256]{2,1,0:T(8,128)(2,1)S(1)}, u32[]{:S(2)}, u32[]{:S(2)}) %all-to-all-start.1) | async-done | bytes 524320 | tf_op jit(solution)/shard_map/all_to_all | solution.py:47
  374.6 7.9 %all_to_all.27 = f32[8,1,128]{2,1,0:T(1,128)S(1)} all-to-all(f32[8,1,128]{2,1,0:T(1,128)S(1)} %broadcast_in_dim.110), channel_id=1, replica_groups=mesh['seq'=16,'head'=8] {'head'}, dimensions={0} | all-to-all | bytes 8192 | tf_op jit(solution)/shard_map/all_to_all | solution.py:18
  382.7 12.4 %all_to_all.28 = bf16[8,128,256]{1,2,0:T(8,128)(2,1)S(1)} all-to-all(bf16[8,128,256]{1,2,0:T(8,128)(2,1)S(1)} %broadcast_in_dim.111), channel_id=1, replica_groups=mesh['seq'=16,'head'=8] {'head'}, dimensions={0} | all-to-all | bytes 1048576 | tf_op jit(solution)/shard_map/all_to_all | solution.py:18
  397.9 1.6 fusion.35
  399.6 1.6 convolution_convert_fusion.7
  401.2 36.8 %all-gather.2.cloned.1.call-done = bf16[2048,512]{1,0:T(8,128)(2,1)} async-done(((bf16[128,512]{1,0:T(8,128)(2,1)}), bf16[2048,512]{1,0:T(8,128)(2,1)}) %all-gather.2.cloned.1.call-update) | async-done | bytes 2097168 | tf_op jit(solution)/shard_map/all_gather | solution.py:69
  437.9 37.6 %conditional.1 = (f32[2,128]{1,0:T(2,128)S(1)}, f32[2,128,128]{1,2,0:T(8,128)}) conditional(s32[]{:T(128)} %convert_element_type.124, () %tuple.18, (s32[2048]{0:T(1024)S(1)}, s32[128]{0:T(128)S(1)}, bf16[128,256]{1,0:T(8,128)(2,1)S(1)}, bf16[2048,512]{1,0:T(8,128)(2,1)}, s32[2048]{0:T(1024)S(1)}, /*index=5*/s32[2048]{0:T(1024)S(1)}, ...), branch_computations={%region_12.13_spmd, %region_13.16_spmd} | conditional | flops 275009280 | bytes 45337160 | solution.py:238
  437.9 2.9 copy.142
  443.6 8.6 %copy.143 = f32[2,128,2048]{1,0,2:T(2,128)} copy(f32[2,128,2048]{1,2,0:T(8,128)S(1)} %copy-done.3) | data formatting | bytes 4194304 | tf_op jit(solution)/shard_map
  452.2 16.1 %gather_fusion = f32[2048,2,128]{2,1,0:T(2,128)} fusion(f32[2,128,2048]{1,0,2:T(2,128)} %copy.143, s32[2048]{0:T(1024)S(1)} %fusion.12), kind=kCustom, calls=%fused_computation | custom fusion | bytes 4202496 | tf_op jit(solution)/shard_map/cond/branch_1_fun/jit(_take)/gather | solution.py:227
  468.2 4.2 copy.125
  472.4 3.1 fusion.6
  476.5 1.6 convolution_convert_fusion.3
  478.1 15.6 %all_to_all.29 = bf16[8,128,256]{2,1,0:T(8,128)(2,1)S(1)} all-to-all(bf16[8,128,256]{2,1,0:T(8,128)(2,1)S(1)} %bitcast.163), channel_id=1, replica_groups=mesh['seq'=16,'head'=8] {'head'}, dimensions={0} | all-to-all | bytes 1048576 | tf_op jit(solution)/shard_map/all_to_all | solution.py:47
  (120 shorter events, 29.4 us)
Async XLA Ops:
  6.5 7.1 %copy-start = (bf16[2048,256]{1,0:T(8,128)(2,1)S(1)}, bf16[2048,256]{1,0:T(8,128)(2,1)}, u32[]{:S(2)}) copy-start(bf16[2048,256]{1,0:T(8,128)(2,1)} %param.17) | copy-start | bytes 3145732
  6.5 108.2 %all-reduce.2.cloned.1.call-start = ((), (), s32[]{:S(2)}) async-start(), calls=%async_computation.6 | async-start | bytes 4194304 | tf_op jit(solution)/shard_map/psum | solution.py:13
  21.4 333.0 %reduce-scatter.2.cloned.1.call-start = ((), (), s32[]{:S(2)}) async-start(), calls=%async_computation.7 | async-start | bytes 2228224 | tf_op jit(solution)/shard_map/reduce_scatter | solution.py:33
  21.6 7.6 %copy-start.10 = (bf16[2048,256]{1,0:T(8,128)(2,1)S(1)}, bf16[2048,256]{1,0:T(8,128)(2,1)}, u32[]{:S(2)}) copy-start(bf16[2048,256]{1,0:T(8,128)(2,1)} %param.19) | copy-start | bytes 3145732
  136.1 6.7 %copy-start.2 = (s32[2,512,2048]{2,1,0:T(8,128)S(1)}, s32[2,512,2048]{2,1,0:T(8,128)}, u32[]{:S(2)}) copy-start(s32[2,512,2048]{2,1,0:T(8,128)} %shift_right_arithmetic.115) | copy-start | bytes 25165828 | tf_op jit(solution)/shard_map/while
  172.0 6.7 %copy-start.2 = (s32[2,512,2048]{2,1,0:T(8,128)S(1)}, s32[2,512,2048]{2,1,0:T(8,128)}, u32[]{:S(2)}) copy-start(s32[2,512,2048]{2,1,0:T(8,128)} %shift_right_arithmetic.115) | copy-start | bytes 25165828 | tf_op jit(solution)/shard_map/while
  207.9 6.7 %copy-start.2 = (s32[2,512,2048]{2,1,0:T(8,128)S(1)}, s32[2,512,2048]{2,1,0:T(8,128)}, u32[]{:S(2)}) copy-start(s32[2,512,2048]{2,1,0:T(8,128)} %shift_right_arithmetic.115) | copy-start | bytes 25165828 | tf_op jit(solution)/shard_map/while
  243.9 6.7 %copy-start.2 = (s32[2,512,2048]{2,1,0:T(8,128)S(1)}, s32[2,512,2048]{2,1,0:T(8,128)}, u32[]{:S(2)}) copy-start(s32[2,512,2048]{2,1,0:T(8,128)} %shift_right_arithmetic.115) | copy-start | bytes 25165828 | tf_op jit(solution)/shard_map/while
  275.9 80.5 %copy-start.6 = (bf16[256,2048]{1,0:T(8,128)(2,1)S(1)}, bf16[256,2048]{1,0:T(8,128)(2,1)}, u32[]{:S(2)}) copy-start(bf16[256,2048]{1,0:T(8,128)(2,1)} %param.20) | copy-start | bytes 3145732
  356.7 38.3 %copy-start.7 = (bf16[2048,256]{1,0:T(8,128)(2,1)S(1)}, bf16[2048,256]{1,0:T(8,128)(2,1)}, u32[]{:S(2)}) copy-start(bf16[2048,256]{1,0:T(8,128)(2,1)} %param.23) | copy-start | bytes 3145732
  357.6 15.9 %all-to-all-start.1 = ((bf16[8,128,256]{2,1,0:T(8,128)(2,1)}), bf16[8,128,256]{2,1,0:T(8,128)(2,1)S(1)}, u32[]{:S(2)}, u32[]{:S(2)}) async-start(bf16[8,128,256]{2,1,0:T(8,128)(2,1)} %bitcast.136), calls=%async_computation.2 | async-start | bytes 1048576 | tf_op jit(solution)/shard_map/all_to_all | solution.py:47
  364.2 31.3 %copy-start.8 = (bf16[2048,256]{1,0:T(8,128)(2,1)S(1)}, bf16[2048,256]{1,0:T(8,128)(2,1)}, u32[]{:S(2)}) copy-start(bf16[2048,256]{1,0:T(8,128)(2,1)} %param.22) | copy-start | bytes 3145732
  364.2 73.8 %all-gather.2.cloned.1.call-start = ((), (), s32[]{:S(2)}) async-start(), calls=%async_computation.8 | async-start | bytes 2228224 | tf_op jit(solution)/shard_map/all_gather | solution.py:69
  365.8 16.7 %copy-start.4 = (f32[2,128,256]{1,2,0:T(8,128)}, f32[2,128,256]{1,2,0:T(8,128)S(1)}, u32[]{:S(2)}) copy-start(f32[2,128,256]{1,2,0:T(8,128)S(1)} %fusion.37) | copy-start | bytes 786436
  440.9 2.7 copy-start.3
  452.2 20.2 %copy-start.9 = (bf16[2048,256]{0,1:T(8,128)(2,1)S(1)}, bf16[2048,256]{0,1:T(8,128)(2,1)}, u32[]{:S(2)}) copy-start(bf16[2048,256]{0,1:T(8,128)(2,1)} %get-tuple-element.237) | copy-start | bytes 3145732 | tf_op jit(solution)/shard_map/cond
  475.5 18.4 %copy-start.5 = (f32[2,128,256]{1,2,0:T(8,128)S(1)}, f32[2,128,256]{1,2,0:T(8,128)}, u32[]{:S(2)}) copy-start(f32[2,128,256]{1,2,0:T(8,128)} %copy-done.4) | copy-start | bytes 786436
  475.5 19.2 %copy-start.1 = (bf16[2048,256]{1,0:T(8,128)(2,1)S(1)}, bf16[2048,256]{1,0:T(8,128)(2,1)}, u32[]{:S(2)}) copy-start(bf16[2048,256]{1,0:T(8,128)(2,1)} %param.17) | copy-start | bytes 3145732
Sparse Core Ops, SparseCore 0:
  21.5 93.1 all-reduce.1
  279.8 74.4 reduce-scatter.1
  396.7 41.2 all-gather.1
where the time goes:
time: 503 us; the launch traced here: 501 us
  waiting for transfers between devices  197 us (39%)
  local copies, waits for them, and re-layouts  107 us (21%)
  matrix products  84.7 us (17%)
  blocking collectives  47.5 us (9%)
  other arithmetic  41.3 us (8%)
  between operations  14.1 us (3%)
  starting transfers between devices  6.82 us (1%)
    psum x1, waiting for transfers between devices, from_root(): return lax.psum(kept, axis)  78.3 us
    reduce_scatter x1, waiting for transfers between devices, side_by_side(): filled = lax.psum_scatter(both, axis, scatter_dimension=dim, tiled=True)  74.6 us
    shift_right_arithmetic x14, local copies, waits for them, and re-layouts, unpack_bits(): jnp.right_shift(packed_words[..., None, :], shifts[:, None])  57.7 us
    all_gather x1, waiting for transfers between devices, side_by_side_2(): filled = lax.all_gather(both, axis, axis=dim, tiled=True)  36.8 us
    dot_general x4, matrix products, cross_block(): jnp.einsum('hqk,khd->hqd', weights, value_heads, preferred_element_type=j...  32.1 us
    all_to_all x3, blocking collectives, copy_for_each(): lax.all_to_all(jnp.broadcast_to(value[None], (size, *value.shape)), axis,...  31.9 us
    dot_general x4, matrix products, cross_block(): jnp.einsum('qhd,khd->hqk', query_block, key_heads, preferred_element_type...  26.5 us
    gather x2, local copies, waits for them, and re-layouts, update(): keep_flags = jnp.take(latent_mask, key_index, axis=2)  20.2 us
  transfers between devices with their start and end apart: 4, of which 4 were waited for; matrix products, arithmetic and copies ran while one was open for 4% of the time, Pallas kernels for 0%

commit v1 on v0

--- a/solution.py
+++ b/solution.py
@@ -6,11 +6,12 @@
 
 keep_scale = 8.0 / 7.0
 masked = -1e30
+_match_fields = lambda unit, which_axis: lax.all_gather(unit, which_axis).sum(axis=0)
 
 
 def from_root(value, axis, source):
     kept = jnp.where(lax.axis_index(axis) == source, value, 0).astype(value.dtype)
-    return lax.psum(kept, axis)
+    return _match_fields(kept, axis)
 
 
 def copy_for_each(value, axis):

time: 503 us -> 601 us (1.19)
  waiting for transfers between devices: 197 us -> 302 us
  matrix products: 84.7 us -> 73.6 us
    all_gather x0 -> x1, waiting for transfers between devices: none -> 185 us  [lax.all_gather(unit, which_axis).sum(axis=0)]
    psum x1 -> x0, waiting for transfers between devices: 78.3 us -> none  [from_root(): return lax.psum(kept, axis)]
    dot_general x4, matrix products: 26.5 us -> 13.2 us  [cross_block(): jnp.einsum('qhd,khd->hqk', query_block, key_heads, preferred_element_type...]
    reduce_sum x0 -> x1, other arithmetic: none -> 11.6 us  [lax.all_gather(unit, which_axis).sum(axis=0)]
    reduce_sum x4, other arithmetic: 20 us -> 11.3 us  [cross_block(): row_sum = jnp.sum(exponent, axis=-1)]
where the time goes in v1:
time: 601 us; the launch traced here: 599 us
  waiting for transfers between devices  302 us (50%)
  local copies, waits for them, and re-layouts  110 us (18%)
  matrix products  73.6 us (12%)
  blocking collectives  48.3 us (8%)
  other arithmetic  42.1 us (7%)
  between operations  14.1 us (2%)
  starting transfers between devices  6.76 us (1%)
    all_gather x1, waiting for transfers between devices, lax.all_gather(unit, which_axis).sum(axis=0)  185 us
    reduce_scatter x1, waiting for transfers between devices, side_by_side(): filled = lax.psum_scatter(both, axis, scatter_dimension=dim, tiled=True)  72.9 us
    shift_right_arithmetic x14, local copies, waits for them, and re-layouts, unpack_bits(): jnp.right_shift(packed_words[..., None, :], shifts[:, None])  57.9 us
    all_gather x1, waiting for transfers between devices, side_by_side_2(): filled = lax.all_gather(both, axis, axis=dim, tiled=True)  36.8 us
    dot_general x4, matrix products, cross_block(): jnp.einsum('hqk,khd->hqd', weights, value_heads, preferred_element_type=j...  34.2 us
    all_to_all x3, blocking collectives, copy_for_each(): lax.all_to_all(jnp.broadcast_to(value[None], (size, *value.shape)), axis,...  32.7 us
    gather x2, local copies, waits for them, and re-layouts, update(): keep_flags = jnp.take(latent_mask, key_index, axis=2)  20.2 us
    all_to_all x1, blocking collectives, sum_at_owner(): lax.all_to_all(parts, axis, split_axis=0, concat_axis=0, tiled=True)  15.6 us
  transfers between devices with their start and end apart: 4, of which 4 were waited for; matrix products, arithmetic and copies ran while one was open for 4% of the time, Pallas kernels for 0%

profile of v1, /device:TPU:1, one launch (start us, length us, event | category | flops | bytes accessed | tf_op | source)
XLA Modules:
  0.0 599.3 jit_solution(17042551040777457872)
XLA Ops:
  6.5 5.2 fusion.28
  14.5 6.0 fusion.30
  20.9 2.5 copy.145
  23.6 6.2 %convolution_convert_fusion.1 = bf16[2048,256]{0,1:T(8,128)(2,1)S(1)} fusion(bf16[2048,256]{1,0:T(8,128)(2,1)} %param.18, bf16[2048,2048]{1,0:T(8,128)(2,1)} %param.16, f32[2048]{0:T(1024)S(1)} %add_rsqrt_fusion), kind=kOutput, calls=%fused_computation.52 | convolution fusion | flops 2160590848 | bytes 10493952 | tf_op jit(solution)/shard_map/dot_general | solution.py:112
  29.8 1.5 copy.149
  31.3 5.9 convolution_convert_fusion
  38.5 185.3 %all-gather.3.cloned.1.call-done = bf16[16,2048,512]{2,1,0:T(8,128)(2,1)} async-done(((bf16[1,2048,512]{2,1,0:T(8,128)(2,1)}), bf16[16,2048,512]{2,1,0:T(8,128)(2,1)}) %all-gather.3.cloned.1.call-update) | async-done | bytes 33554448 | tf_op jit(solution)/shard_map/all_gather | solution.py:9
  223.8 11.6 %reduce_sum.76 = bf16[2048,512]{1,0:T(8,128)(2,1)S(1)} reduce(bf16[16,2048,512]{2,1,0:T(8,128)(2,1)} %all-gather.3.cloned.1.call-done, bf16[]{:T(256)} %constant.99.clone.1), dimensions={0}, to_apply=%region_1.2 | reduce | flops 15728640 | bytes 35651584 | tf_op jit(solution)/shard_map/reduce_sum | solution.py:9
  236.9 126.4 %while.15 = (s32[]{:T(128)}, f32[4,2,512,128]{3,2,0,1:T(8,128)}, f32[4,2,512]{2,1,0:T(2,128)S(1)}, f32[4,2,512]{2,1,0:T(2,128)S(1)}, s32[4]{0:T(128)S(1)}, /*ind...) while((s32[]{:T(128)}, f32[4,2,512,128]{3,2,0,1:T(8,128)}, ...), condition=%wide.region_5.6_spmd.clone, body=%wide.region_2.5_spmd.clone.sunk | while | flops 1112539648 | bytes 107303664 | solution.py:148
  239.0 3.3 fusion.82
  242.3 2.8 fusion.84
  246.8 3.8 shift_right_arithmetic.114
  250.6 9.4 %shift_right_arithmetic.115 = s32[2,512,2048]{2,1,0:T(8,128)} reshape(s32[2,512,8,256]{3,2,1,0:T(8,128)} %shift_right_arithmetic.114) | data formatting | bytes 16777216 | tf_op jit(solution)/shard_map/while/body/eval_jaxpr/shift_right_arithmetic | solution.py:76
  260.0 8.5 %fusion.83 = f32[4,2,512,128]{3,2,0,1:T(8,128)} fusion(f32[4,2,512,128]{3,2,0,1:T(8,128)} %get-tuple-element.342, s32[]{:T(128)} %get-tuple-element.341, bf16[2048,2,128]{2,0,1:T(8,128)(2,1)S(1)} %copy-done.10, s32[2,512,2048]{2,1,0:T(8,128)} %shift_right_arithmetic.115, f32[2,512,2048]{2,1,0:T(8,128)} %copy-done.2, s32[2048]{0:T(1024)S(1)} %bitcast.171, ...), kind=kOutput, calls=%fused_computation.32.clone.1 | convolution fusion | flops 557842432 | bytes 19411456 | tf_op jit(solution)/shard_map/while/body/eval_jaxpr/hqk,khd->hqd/dot_general | solution.py:143
  270.6 3.3 fusion.82
  273.9 2.8 fusion.84
  278.4 3.8 shift_right_arithmetic.114
  282.2 9.4 %shift_right_arithmetic.115 = s32[2,512,2048]{2,1,0:T(8,128)} reshape(s32[2,512,8,256]{3,2,1,0:T(8,128)} %shift_right_arithmetic.114) | data formatting | bytes 16777216 | tf_op jit(solution)/shard_map/while/body/eval_jaxpr/shift_right_arithmetic | solution.py:76
  291.6 8.6 %fusion.83 = f32[4,2,512,128]{3,2,0,1:T(8,128)} fusion(f32[4,2,512,128]{3,2,0,1:T(8,128)} %get-tuple-element.342, s32[]{:T(128)} %get-tuple-element.341, bf16[2048,2,128]{2,0,1:T(8,128)(2,1)S(1)} %copy-done.10, s32[2,512,2048]{2,1,0:T(8,128)} %shift_right_arithmetic.115, f32[2,512,2048]{2,1,0:T(8,128)} %copy-done.2, s32[2048]{0:T(1024)S(1)} %bitcast.171, ...), kind=kOutput, calls=%fused_computation.32.clone.1 | convolution fusion | flops 557842432 | bytes 19411456 | tf_op jit(solution)/shard_map/while/body/eval_jaxpr/hqk,khd->hqd/dot_general | solution.py:143
  302.2 3.3 fusion.82
  305.5 2.8 fusion.84
  310.0 3.8 shift_right_arithmetic.114
  313.8 9.4 %shift_right_arithmetic.115 = s32[2,512,2048]{2,1,0:T(8,128)} reshape(s32[2,512,8,256]{3,2,1,0:T(8,128)} %shift_right_arithmetic.114) | data formatting | bytes 16777216 | tf_op jit(solution)/shard_map/while/body/eval_jaxpr/shift_right_arithmetic | solution.py:76
  323.2 8.5 %fusion.83 = f32[4,2,512,128]{3,2,0,1:T(8,128)} fusion(f32[4,2,512,128]{3,2,0,1:T(8,128)} %get-tuple-element.342, s32[]{:T(128)} %get-tuple-element.341, bf16[2048,2,128]{2,0,1:T(8,128)(2,1)S(1)} %copy-done.10, s32[2,512,2048]{2,1,0:T(8,128)} %shift_right_arithmetic.115, f32[2,512,2048]{2,1,0:T(8,128)} %copy-done.2, s32[2048]{0:T(1024)S(1)} %bitcast.171, ...), kind=kOutput, calls=%fused_computation.32.clone.1 | convolution fusion | flops 557842432 | bytes 19411456 | tf_op jit(solution)/shard_map/while/body/eval_jaxpr/hqk,khd->hqd/dot_general | solution.py:143
  333.8 3.3 fusion.82
  337.1 2.8 fusion.84
  341.6 3.8 shift_right_arithmetic.114
  345.4 9.4 %shift_right_arithmetic.115 = s32[2,512,2048]{2,1,0:T(8,128)} reshape(s32[2,512,8,256]{3,2,1,0:T(8,128)} %shift_right_arithmetic.114) | data formatting | bytes 16777216 | tf_op jit(solution)/shard_map/while/body/eval_jaxpr/shift_right_arithmetic | solution.py:76
  354.8 8.6 %fusion.83 = f32[4,2,512,128]{3,2,0,1:T(8,128)} fusion(f32[4,2,512,128]{3,2,0,1:T(8,128)} %get-tuple-element.342, s32[]{:T(128)} %get-tuple-element.341, bf16[2048,2,128]{2,0,1:T(8,128)(2,1)S(1)} %copy-done.10, s32[2,512,2048]{2,1,0:T(8,128)} %shift_right_arithmetic.115, f32[2,512,2048]{2,1,0:T(8,128)} %copy-done.2, s32[2048]{0:T(1024)S(1)} %bitcast.171, ...), kind=kOutput, calls=%fused_computation.32.clone.1 | convolution fusion | flops 557842432 | bytes 19411456 | tf_op jit(solution)/shard_map/while/body/eval_jaxpr/hqk,khd->hqd/dot_general | solution.py:143
  363.5 12.3 %all_to_all.26 = f32[16,2,2048]{2,1,0:T(2,128)S(1)} all-to-all(f32[16,2,2048]{2,1,0:T(2,128)S(1)} %broadcast_in_dim.109), channel_id=1, replica_groups=mesh['seq'=16,'head'=8] {'seq'}, dimensions={0} | all-to-all | bytes 524288 | tf_op jit(solution)/shard_map/all_to_all | solution.py:19
  376.5 2.0 fusion.31
  378.5 1.8 pad_maximum_fusion
  380.3 72.9 %reduce-scatter.2.cloned.1.call-done = bf16[2,128,129]{2,1,0:T(8,128)(2,1)} async-done(((bf16[2,2048,129]{2,1,0:T(8,128)(2,1)}), bf16[2,128,129]{2,1,0:T(8,128)(2,1)}) %reduce-scatter.2.cloned.1.call-update) | async-done | bytes 66064 | tf_op jit(solution)/shard_map/reduce_scatter | solution.py:34
  456.3 6.7 %all-to-all-start.1 = ((bf16[8,128,256]{2,1,0:T(8,128)(2,1)}), bf16[8,128,256]{2,1,0:T(8,128)(2,1)S(1)}, u32[]{:S(2)}, u32[]{:S(2)}) async-start(bf16[8,128,256]{2,1,0:T(8,128)(2,1)} %bitcast.137), calls=%async_computation.2 | async-start | bytes 1048576 | tf_op jit(solution)/shard_map/all_to_all | solution.py:48
  465.7 6.7 %all-to-all-done.1 = bf16[8,128,256]{2,1,0:T(8,128)(2,1)S(1)} async-done(((bf16[8,128,256]{2,1,0:T(8,128)(2,1)}), bf16[8,128,256]{2,1,0:T(8,128)(2,1)S(1)}, u32[]{:S(2)}, u32[]{:S(2)}) %all-to-all-start.1) | async-done | bytes 524320 | tf_op jit(solution)/shard_map/all_to_all | solution.py:48
  472.6 7.9 %all_to_all.27 = f32[8,1,128]{2,1,0:T(1,128)S(1)} all-to-all(f32[8,1,128]{2,1,0:T(1,128)S(1)} %broadcast_in_dim.110), channel_id=1, replica_groups=mesh['seq'=16,'head'=8] {'head'}, dimensions={0} | all-to-all | bytes 8192 | tf_op jit(solution)/shard_map/all_to_all | solution.py:19
  480.7 12.4 %all_to_all.28 = bf16[8,128,256]{1,2,0:T(8,128)(2,1)S(1)} all-to-all(bf16[8,128,256]{1,2,0:T(8,128)(2,1)S(1)} %broadcast_in_dim.111), channel_id=1, replica_groups=mesh['seq'=16,'head'=8] {'head'}, dimensions={0} | all-to-all | bytes 1048576 | tf_op jit(solution)/shard_map/all_to_all | solution.py:19
  495.3 1.6 fusion.33
  497.6 1.6 convolution_convert_fusion.7
  499.2 36.8 %all-gather.5.cloned.1.call-done = bf16[2048,512]{1,0:T(8,128)(2,1)} async-done(((bf16[128,512]{1,0:T(8,128)(2,1)}), bf16[2048,512]{1,0:T(8,128)(2,1)}) %all-gather.5.cloned.1.call-update) | async-done | bytes 2097168 | tf_op jit(solution)/shard_map/all_gather | solution.py:70
  536.0 37.6 %conditional.1 = (f32[2,128]{1,0:T(2,128)S(1)}, f32[2,128,128]{1,2,0:T(8,128)}) conditional(s32[]{:T(128)} %convert_element_type.126, () %tuple.18, (s32[2048]{0:T(1024)S(1)}, s32[128]{0:T(128)S(1)}, bf16[128,256]{1,0:T(8,128)(2,1)S(1)}, bf16[2048,512]{1,0:T(8,128)(2,1)}, s32[2048]{0:T(1024)S(1)}, /*index=5*/s32[2048]{0:T(1024)S(1)}, ...), branch_computations={%region_12.13_spmd, %region_13.16_spmd} | conditional | flops 275009280 | bytes 45337160 | solution.py:239
  536.2 2.9 copy.160
  541.1 8.6 %copy.161 = f32[2,128,2048]{1,0,2:T(2,128)} copy(f32[2,128,2048]{1,2,0:T(8,128)S(1)} %copy-done.3) | data formatting | bytes 4194304 | tf_op jit(solution)/shard_map
  549.7 16.1 %gather_fusion = f32[2048,2,128]{2,1,0:T(2,128)} fusion(f32[2,128,2048]{1,0,2:T(2,128)} %copy.161, s32[2048]{0:T(1024)S(1)} %fusion.12), kind=kCustom, calls=%fused_computation | custom fusion | bytes 4202496 | tf_op jit(solution)/shard_map/cond/branch_1_fun/jit(_take)/gather | solution.py:228
  565.7 4.2 copy.142
  569.9 3.1 fusion.6
  574.6 1.6 convolution_convert_fusion.3
  576.2 15.6 %all_to_all.29 = bf16[8,128,256]{2,1,0:T(8,128)(2,1)S(1)} all-to-all(bf16[8,128,256]{2,1,0:T(8,128)(2,1)S(1)} %bitcast.165), channel_id=1, replica_groups=mesh['seq'=16,'head'=8] {'head'}, dimensions={0} | all-to-all | bytes 1048576 | tf_op jit(solution)/shard_map/all_to_all | solution.py:48
  (137 shorter events, 32.4 us)
Async XLA Ops:
  6.5 7.9 %copy-start = (bf16[2048,256]{1,0:T(8,128)(2,1)S(1)}, bf16[2048,256]{1,0:T(8,128)(2,1)}, u32[]{:S(2)}) copy-start(bf16[2048,256]{1,0:T(8,128)(2,1)} %param.17) | copy-start | bytes 3145732
  6.5 217.2 %all-gather.3.cloned.1.call-start = ((), (), s32[]{:S(2)}) async-start(), calls=%async_computation.6 | async-start | bytes 35651584 | tf_op jit(solution)/shard_map/all_gather | solution.py:9
  14.5 6.0 %copy-start.4 = (bf16[2048,256]{0,1:T(8,128)(2,1)S(1)}, bf16[2048,256]{0,1:T(8,128)(2,1)}, u32[]{:S(2)}) copy-start(bf16[2048,256]{0,1:T(8,128)(2,1)} %copy.144) | copy-start | bytes 3145732
  23.5 429.7 %reduce-scatter.2.cloned.1.call-start = ((), (), s32[]{:S(2)}) async-start(), calls=%async_computation.7 | async-start | bytes 2228224 | tf_op jit(solution)/shard_map/reduce_scatter | solution.py:34
  23.5 7.7 %copy-start.12 = (bf16[2048,256]{1,0:T(8,128)(2,1)S(1)}, bf16[2048,256]{1,0:T(8,128)(2,1)}, u32[]{:S(2)}) copy-start(bf16[2048,256]{1,0:T(8,128)(2,1)} %param.19) | copy-start | bytes 3145732
  242.3 3.2 copy-start.2
  250.6 9.4 %copy-start.10 = (bf16[2048,2,128]{2,0,1:T(8,128)(2,1)S(1)}, bf16[2048,2,128]{2,0,1:T(8,128)(2,1)}, u32[]{:S(2)}) copy-start(bf16[2048,2,128]{2,0,1:T(8,128)(2,1)} %get-tuple-element.362) | copy-start | bytes 3145732 | tf_op jit(solution)/shard_map/while
  273.9 3.2 copy-start.2
  282.2 9.4 %copy-start.10 = (bf16[2048,2,128]{2,0,1:T(8,128)(2,1)S(1)}, bf16[2048,2,128]{2,0,1:T(8,128)(2,1)}, u32[]{:S(2)}) copy-start(bf16[2048,2,128]{2,0,1:T(8,128)(2,1)} %get-tuple-element.362) | copy-start | bytes 3145732 | tf_op jit(solution)/shard_map/while
  305.5 3.2 copy-start.2
  313.8 9.4 %copy-start.10 = (bf16[2048,2,128]{2,0,1:T(8,128)(2,1)S(1)}, bf16[2048,2,128]{2,0,1:T(8,128)(2,1)}, u32[]{:S(2)}) copy-start(bf16[2048,2,128]{2,0,1:T(8,128)(2,1)} %get-tuple-element.362) | copy-start | bytes 3145732 | tf_op jit(solution)/shard_map/while
  337.1 3.2 copy-start.2
  345.4 9.4 %copy-start.10 = (bf16[2048,2,128]{2,0,1:T(8,128)(2,1)S(1)}, bf16[2048,2,128]{2,0,1:T(8,128)(2,1)}, u32[]{:S(2)}) copy-start(bf16[2048,2,128]{2,0,1:T(8,128)(2,1)} %get-tuple-element.362) | copy-start | bytes 3145732 | tf_op jit(solution)/shard_map/while
  376.5 78.7 %copy-start.7 = (bf16[256,2048]{1,0:T(8,128)(2,1)S(1)}, bf16[256,2048]{1,0:T(8,128)(2,1)}, u32[]{:S(2)}) copy-start(bf16[256,2048]{1,0:T(8,128)(2,1)} %param.20) | copy-start | bytes 3145732
  456.3 36.8 %copy-start.8 = (bf16[2048,256]{1,0:T(8,128)(2,1)S(1)}, bf16[2048,256]{1,0:T(8,128)(2,1)}, u32[]{:S(2)}) copy-start(bf16[2048,256]{1,0:T(8,128)(2,1)} %param.23) | copy-start | bytes 3145732
  456.3 16.1 %all-to-all-start.1 = ((bf16[8,128,256]{2,1,0:T(8,128)(2,1)}), bf16[8,128,256]{2,1,0:T(8,128)(2,1)S(1)}, u32[]{:S(2)}, u32[]{:S(2)}) async-start(bf16[8,128,256]{2,1,0:T(8,128)(2,1)} %bitcast.137), calls=%async_computation.2 | async-start | bytes 1048576 | tf_op jit(solution)/shard_map/all_to_all | solution.py:48
  463.1 30.4 %copy-start.9 = (bf16[2048,256]{1,0:T(8,128)(2,1)S(1)}, bf16[2048,256]{1,0:T(8,128)(2,1)}, u32[]{:S(2)}) copy-start(bf16[2048,256]{1,0:T(8,128)(2,1)} %param.22) | copy-start | bytes 3145732
  463.1 72.9 %all-gather.5.cloned.1.call-start = ((), (), s32[]{:S(2)}) async-start(), calls=%async_computation.8 | async-start | bytes 2228224 | tf_op jit(solution)/shard_map/all_gather | solution.py:70
  464.7 15.9 %copy-start.5 = (f32[2,128,256]{1,2,0:T(8,128)}, f32[2,128,256]{1,2,0:T(8,128)S(1)}, u32[]{:S(2)}) copy-start(f32[2,128,256]{1,2,0:T(8,128)S(1)} %fusion.35) | copy-start | bytes 786436
  539.1 2.0 copy-start.3
  549.7 20.2 %copy-start.11 = (bf16[2048,256]{0,1:T(8,128)(2,1)S(1)}, bf16[2048,256]{0,1:T(8,128)(2,1)}, u32[]{:S(2)}) copy-start(bf16[2048,256]{0,1:T(8,128)(2,1)} %get-tuple-element.247) | copy-start | bytes 3145732 | tf_op jit(solution)/shard_map/cond
  573.6 18.4 %copy-start.6 = (f32[2,128,256]{1,2,0:T(8,128)S(1)}, f32[2,128,256]{1,2,0:T(8,128)}, u32[]{:S(2)}) copy-start(f32[2,128,256]{1,2,0:T(8,128)} %copy-done.5) | copy-start | bytes 786436
  573.6 19.2 %copy-start.1 = (bf16[2048,256]{1,0:T(8,128)(2,1)S(1)}, bf16[2048,256]{1,0:T(8,128)(2,1)}, u32[]{:S(2)}) copy-start(bf16[2048,256]{1,0:T(8,128)(2,1)} %param.17) | copy-start | bytes 3145732
Sparse Core Ops, SparseCore 0:
  23.6 200.1 all-gather.2
  380.4 72.6 reduce-scatter.1
  494.7 41.2 all-gather.4
